TPU v7x, 512 devices: a whole 4x8x8 slice. The times are simulated.
512 devices in a mesh: bank: 4 (over z_hi), lane: 16 (over y, core), site: 8 (over z_lo, x).
Axes of the slice: x: 4, y: 8, z: 8 (z_hi: 4, z_lo: 2; z = z_hi * 2 + z_lo), core: 2. Of those that a mesh axis runs over, the one named last changes fastest.
Arguments:
- wave_parts: float32 [16, 256, 128, 128], P('site', ('bank', 'lane')), parts along dimension 0, may hold values from -6 to 6
- level_table: float32 [2048, 128, 128], P(('site', 'bank', 'lane')), parts along dimension 0, may hold values from -2 to 2
- phase_angles: float32 [16, 128], P('site'), parts along dimension 0, may hold values from 0.3 to 1.2
- mix_angles: float32 [16, 4], P('site'), parts along dimension 0, may hold values from 0.3 to 1.2
Outputs:
- final_parts: float32 [16, 256, 128, 128], P('site', ('bank', 'lane')), parts along dimension 0
There are 8 independent parts, one for each index of `site`. A program takes and returns all parts, laid end to end along the dimension named above; each array names one. Nothing has to cross between parts.
All inputs are finite; a program needn't handle non-finite values.
Results may differ from a plain program's by a relative error of at most 0.0003.
Values sent between devices are 32-bit elements; how exact they have to be, the bound alone decides.
No kernel may reach another device: no remote copies, remote signals or barrier semaphores. Data moves between devices by JAX's collectives and lax.ppermute only.
A program may use at most 64 MiB of HBM per device.

v0:
```python
import jax
import jax.numpy as jnp
from jax import lax
from jax.sharding import PartitionSpec as P

LAYERS = 2


def count_bits(values, count):
    places = jnp.arange(count.bit_length() - 1, dtype=jnp.int32)
    return jnp.sum(values[..., None] >> places & 1, axis=-1)


def plane_table(count, angle):
    rank = jnp.arange(count, dtype=jnp.int32)
    apart = count_bits(rank[:, None] ^ rank[None, :], count)
    minus = count_bits(rank[:, None] & (rank[:, None] ^ rank[None, :]), count)
    bits = count.bit_length() - 1
    size = jnp.cos(angle) ** (bits - apart).astype(jnp.float32) * jnp.sin(angle) ** apart.astype(
        jnp.float32
    )
    return size * jnp.where(minus % 2 == 1, -1.0, 1.0).astype(jnp.float32)


def apply_along(values, dim, angle):
    real_part = plane_table(values.shape[dim], angle)
    moved = jnp.tensordot(values, real_part, axes=([dim], [0]), precision=lax.Precision.HIGHEST)
    return jnp.moveaxis(moved, -1, dim)


def turn_phase(values, levels, angle):
    turn = angle * levels
    return jnp.stack(
        [
            values[0] * jnp.cos(turn) + values[1] * jnp.sin(turn),
            values[1] * jnp.cos(turn) - values[0] * jnp.sin(turn),
        ]
    )


def local(wave_parts, level_table, phase_angles, mix_angles):
    values = wave_parts
    for layer in range(LAYERS):
        values = turn_phase(values, level_table, phase_angles[layer])
        values = apply_along(values, 3, mix_angles[layer, 0])
        values = apply_along(values, 2, mix_angles[layer, 1])
        moved = lax.all_to_all(values, "bank", split_axis=2, concat_axis=1, tiled=True)
        moved = apply_along(moved, 1, mix_angles[layer, 2])
        values = lax.all_to_all(moved, "bank", split_axis=1, concat_axis=2, tiled=True)
        moved = lax.all_to_all(values, "lane", split_axis=3, concat_axis=1, tiled=True)
        spread = moved.reshape(2, lax.axis_size("lane"), -1, moved.shape[2], moved.shape[3])
        moved = apply_along(spread, 1, mix_angles[layer, 3]).reshape(moved.shape)
        values = lax.all_to_all(moved, "lane", split_axis=1, concat_axis=3, tiled=True)
    return values


def solution(mesh):
    placed = (
        P("site", ("bank", "lane"), None, None),
        P(("site", "bank", "lane"), None, None),
        P("site", None),
        P("site", None),
    )
    return jax.shard_map(
        local,
        mesh=mesh,
        in_specs=placed,
        out_specs=P("site", ("bank", "lane"), None, None),
        check_vma=False,
    )
```

profile of v0, /device:TPU:1, one launch (start us, length us, event | category | flops | bytes accessed | tf_op | source)
XLA Modules:
  0.0 193.1 jit_solution(17177056448515997005)
XLA Ops:
  0.0 0.0 copy-start
  0.0 1.7 fusion.151
  4.7 0.0 copy-start.1
  4.7 0.6 copy-done.1
  5.3 0.0 copy-done
  5.4 2.0 %fusion.13 = (f32[1,4,128,128]{3,2,1,0:T(8,128)S(1)}, f32[1,4,128,128]{3,2,1,0:T(8,128)S(1)}) fusion(f32[2,4,128,128]{3,2,1,0:T(8,128)} %param.4, f32[4,128,128]{2,1,0:T(8,128)S(1)} %copy-done, f32[128]{0:T(128)S(1)} %get-tuple-element.20), kind=kLoop, calls=%fused_computation.24 | loop fusion | flops 458752 | bytes 1311232 | tf_op jit(solution)/shard_map/stack | solution.py:33
  7.3 0.8 fusion
  8.2 0.8 convolution_bitcast_fusion.5
  8.9 1.0 copy.89
  9.9 10.8 %all-to-all-start = ((f32[2,4,128,128]{3,1,0,2:T(4,128)}), f32[2,4,128,128]{3,1,0,2:T(4,128)S(1)}, u32[]{:S(2)}, u32[]{:S(2)}) async-start(f32[2,4,128,128]{3,1,0,2:T(4,128)} %copy.89), calls=%async_computation | async-start | bytes 1048576 | tf_op jit(solution)/shard_map/all_to_all | solution.py:47
  22.2 10.4 %all-to-all-done = f32[2,4,128,128]{3,1,0,2:T(4,128)S(1)} async-done(((f32[2,4,128,128]{3,1,0,2:T(4,128)}), f32[2,4,128,128]{3,1,0,2:T(4,128)S(1)}, u32[]{:S(2)}, u32[]{:S(2)}) %all-to-all-start) | async-done | bytes 524320 | tf_op jit(solution)/shard_map/all_to_all | solution.py:47
  32.7 0.1 copy.90
  32.8 0.3 copy.91
  33.1 0.6 convolution_bitcast_fusion.4
  33.8 0.2 copy.93
  34.0 17.1 %all_to_all.135 = f32[2,16,32,128]{3,2,0,1:T(8,128)S(1)} all-to-all(f32[2,16,32,128]{3,2,0,1:T(8,128)S(1)} %copy.93), channel_id=1, replica_groups=mesh['bank'=4,'lane'=16,'site'=8] {'bank'}, dimensions={1} | all-to-all | bytes 1048576 | tf_op jit(solution)/shard_map/all_to_all | solution.py:49
  51.1 1.0 copy.96
  52.1 12.8 %all-to-all-start.2 = ((f32[2,4,128,128]{2,1,0,3:T(4,128)}), f32[2,4,128,128]{2,1,0,3:T(4,128)S(1)}, u32[]{:S(2)}, u32[]{:S(2)}) async-start(f32[2,4,128,128]{2,1,0,3:T(4,128)} %copy.96), calls=%async_computation.2 | async-start | bytes 1048576 | tf_op jit(solution)/shard_map/all_to_all | solution.py:50
  66.3 15.8 %all-to-all-done.2 = f32[2,4,128,128]{2,1,0,3:T(4,128)S(1)} async-done(((f32[2,4,128,128]{2,1,0,3:T(4,128)}), f32[2,4,128,128]{2,1,0,3:T(4,128)S(1)}, u32[]{:S(2)}, u32[]{:S(2)}) %all-to-all-start.2) | async-done | bytes 524320 | tf_op jit(solution)/shard_map/all_to_all | solution.py:50
  82.1 0.9 convolution_bitcast_fusion.3
  83.0 0.2 copy.100
  83.2 0.8 copy.101
  84.0 3.5 %all-to-all-start.3 = ((f32[2,64,128,8]{2,3,0,1:T(8,128)}), f32[2,64,128,8]{2,3,0,1:T(8,128)S(1)}, u32[]{:S(2)}, u32[]{:S(2)}) async-start(f32[2,64,128,8]{2,3,0,1:T(8,128)} %copy.101), calls=%async_computation.3 | async-start | bytes 1048576 | tf_op jit(solution)/shard_map/all_to_all | solution.py:53
  90.4 13.8 %all-to-all-done.3 = f32[2,64,128,8]{2,3,0,1:T(8,128)S(1)} async-done(((f32[2,64,128,8]{2,3,0,1:T(8,128)}), f32[2,64,128,8]{2,3,0,1:T(8,128)S(1)}, u32[]{:S(2)}, u32[]{:S(2)}) %all-to-all-start.3) | async-done | bytes 524320 | tf_op jit(solution)/shard_map/all_to_all | solution.py:53
  104.3 0.1 copy.104
  104.5 0.1 copy.106
  104.6 1.0 add_bitcast_fusion
  105.6 0.8 fusion.4
  106.5 0.8 convolution_bitcast_fusion.2
  107.2 1.0 copy.110
  108.2 3.5 %all-to-all-start.4 = ((f32[2,4,128,128]{3,1,0,2:T(4,128)}), f32[2,4,128,128]{3,1,0,2:T(4,128)S(1)}, u32[]{:S(2)}, u32[]{:S(2)}) async-start(f32[2,4,128,128]{3,1,0,2:T(4,128)} %copy.110), calls=%async_computation.4 | async-start | bytes 1048576 | tf_op jit(solution)/shard_map/all_to_all | solution.py:47
  113.0 11.6 %all-to-all-done.4 = f32[2,4,128,128]{3,1,0,2:T(4,128)S(1)} async-done(((f32[2,4,128,128]{3,1,0,2:T(4,128)}), f32[2,4,128,128]{3,1,0,2:T(4,128)S(1)}, u32[]{:S(2)}, u32[]{:S(2)}) %all-to-all-start.4) | async-done | bytes 524320 | tf_op jit(solution)/shard_map/all_to_all | solution.py:47
  124.6 0.1 copy.111
  124.7 0.3 copy.112
  125.0 0.6 convolution_bitcast_fusion.1
  125.7 0.2 copy.114
  125.9 19.3 %all_to_all.136 = f32[2,16,32,128]{3,2,0,1:T(8,128)S(1)} all-to-all(f32[2,16,32,128]{3,2,0,1:T(8,128)S(1)} %copy.114), channel_id=1, replica_groups=mesh['bank'=4,'lane'=16,'site'=8] {'bank'}, dimensions={1} | all-to-all | bytes 1048576 | tf_op jit(solution)/shard_map/all_to_all | solution.py:49
  145.2 1.0 copy.117
  146.2 7.5 %all-to-all-start.6 = ((f32[2,4,128,128]{2,1,0,3:T(4,128)}), f32[2,4,128,128]{2,1,0,3:T(4,128)S(1)}, u32[]{:S(2)}, u32[]{:S(2)}) async-start(f32[2,4,128,128]{2,1,0,3:T(4,128)} %copy.117), calls=%async_computation.6 | async-start | bytes 1048576 | tf_op jit(solution)/shard_map/all_to_all | solution.py:50
  155.3 15.8 %all-to-all-done.6 = f32[2,4,128,128]{2,1,0,3:T(4,128)S(1)} async-done(((f32[2,4,128,128]{2,1,0,3:T(4,128)}), f32[2,4,128,128]{2,1,0,3:T(4,128)S(1)}, u32[]{:S(2)}, u32[]{:S(2)}) %all-to-all-start.6) | async-done | bytes 524320 | tf_op jit(solution)/shard_map/all_to_all | solution.py:50
  171.0 0.9 convolution_bitcast_fusion
  171.9 0.2 copy.121
  172.2 19.9 %all_to_all.137 = f32[2,64,128,8]{2,3,0,1:T(8,128)S(1)} all-to-all(f32[2,64,128,8]{2,3,0,1:T(8,128)S(1)} %copy.122), channel_id=1, replica_groups=mesh['bank'=4,'lane'=16,'site'=8] {'lane'}, dimensions={1} | all-to-all | bytes 1048576 | tf_op jit(solution)/shard_map/all_to_all | solution.py:53
  192.1 1.0 copy.125
  (18 shorter events, 0.4 us)
Async XLA Ops:
  0.0 5.4 %copy-start = (f32[4,128,128]{2,1,0:T(8,128)S(1)}, f32[4,128,128]{2,1,0:T(8,128)}, u32[]{:S(2)}) copy-start(f32[4,128,128]{2,1,0:T(8,128)} %param.5) | copy-start | bytes 786436
  4.7 0.7 copy-start.1
  9.9 22.7 %all-to-all-start = ((f32[2,4,128,128]{3,1,0,2:T(4,128)}), f32[2,4,128,128]{3,1,0,2:T(4,128)S(1)}, u32[]{:S(2)}, u32[]{:S(2)}) async-start(f32[2,4,128,128]{3,1,0,2:T(4,128)} %copy.89), calls=%async_computation | async-start | bytes 1048576 | tf_op jit(solution)/shard_map/all_to_all | solution.py:47
  52.1 30.0 %all-to-all-start.2 = ((f32[2,4,128,128]{2,1,0,3:T(4,128)}), f32[2,4,128,128]{2,1,0,3:T(4,128)S(1)}, u32[]{:S(2)}, u32[]{:S(2)}) async-start(f32[2,4,128,128]{2,1,0,3:T(4,128)} %copy.96), calls=%async_computation.2 | async-start | bytes 1048576 | tf_op jit(solution)/shard_map/all_to_all | solution.py:50
  84.0 20.2 %all-to-all-start.3 = ((f32[2,64,128,8]{2,3,0,1:T(8,128)}), f32[2,64,128,8]{2,3,0,1:T(8,128)S(1)}, u32[]{:S(2)}, u32[]{:S(2)}) async-start(f32[2,64,128,8]{2,3,0,1:T(8,128)} %copy.101), calls=%async_computation.3 | async-start | bytes 1048576 | tf_op jit(solution)/shard_map/all_to_all | solution.py:53
  108.2 16.3 %all-to-all-start.4 = ((f32[2,4,128,128]{3,1,0,2:T(4,128)}), f32[2,4,128,128]{3,1,0,2:T(4,128)S(1)}, u32[]{:S(2)}, u32[]{:S(2)}) async-start(f32[2,4,128,128]{3,1,0,2:T(4,128)} %copy.110), calls=%async_computation.4 | async-start | bytes 1048576 | tf_op jit(solution)/shard_map/all_to_all | solution.py:47
  146.2 24.8 %all-to-all-start.6 = ((f32[2,4,128,128]{2,1,0,3:T(4,128)}), f32[2,4,128,128]{2,1,0,3:T(4,128)S(1)}, u32[]{:S(2)}, u32[]{:S(2)}) async-start(f32[2,4,128,128]{2,1,0,3:T(4,128)} %copy.117), calls=%async_computation.6 | async-start | bytes 1048576 | tf_op jit(solution)/shard_map/all_to_all | solution.py:50
where the time goes:
time: 194 us; the launch traced here: 193 us
  waiting for transfers between devices  67.4 us (35%)
  blocking collectives  56.3 us (29%)
  starting transfers between devices  38.1 us (20%)
  between operations  11.7 us (6%)
  local copies, waits for them, and re-layouts  10.1 us (5%)
  matrix products  6.27 us (3%)
  other arithmetic  3.22 us (2%)
    all_to_all x2, blocking collectives, local(): lax.all_to_all(moved, 'bank', split_axis=1, concat_axis=2, tiled=True)  36.4 us
    all_to_all x2, waiting for transfers between devices, local(): lax.all_to_all(values, 'lane', split_axis=3, concat_axis=1, tiled=True)  31.6 us
    all_to_all x2, waiting for transfers between devices, local(): lax.all_to_all(values, 'bank', split_axis=2, concat_axis=1, tiled=True)  22 us
    all_to_all x2, starting transfers between devices, local(): lax.all_to_all(values, 'lane', split_axis=3, concat_axis=1, tiled=True)  20.3 us
    all_to_all x1, blocking collectives, local(): lax.all_to_all(moved, 'lane', split_axis=1, concat_axis=3, tiled=True)  19.9 us
    all_to_all x2, starting transfers between devices, local(): lax.all_to_all(values, 'bank', split_axis=2, concat_axis=1, tiled=True)  14.3 us
    all_to_all x1, waiting for transfers between devices, local(): lax.all_to_all(moved, 'lane', split_axis=1, concat_axis=3, tiled=True)  13.8 us
    dot_general x8, matrix products, apply_along(): jnp.tensordot(values, real_part, axes=([dim], [0]), precision=lax.Precisi...  6.27 us
  transfers between devices with their start and end apart: 5, of which 5 were waited for; matrix products, arithmetic and copies ran while one was open for 0% of the time, Pallas kernels for 0%

commit v1 on v0

v1 whole, which is shorter than its diff:
```python
import jax
import jax.numpy as jnp
from jax import lax
from jax.experimental import pallas as pl
from jax.experimental.pallas import tpu as pltpu
from jax.sharding import PartitionSpec as P

SUB = 8
F32 = jnp.float32

SIN = (0.9999999814442071, -0.16666657755521955, 0.008333210982283118, -0.00019834058585468524,
       2.734996203799263e-06, -2.21633008243829e-08)
COS = (0.9999999997000049, -0.4999999949621528, 0.04166665285119409, -0.0013888746708823352,
       2.4794608537121183e-05, -2.7380880775339007e-07, 1.8645524434398867e-09)


def series(z, terms):
    total = z * terms[-1] + terms[-2]
    for term in terms[-3::-1]:
        total = total * z + term
    return total


def cos_sin(x):
    z = x * x
    return series(z, COS), series(z, SIN) * x


def plane_table(cos, sin, left):
    row = lax.broadcasted_iota(jnp.int32, (128, 128), 0)
    col = lax.broadcasted_iota(jnp.int32, (128, 128), 1)
    if left:
        sin = -sin
    table = None
    for bit in range(7):
        at_row, at_col = (row >> bit) & 1, (col >> bit) & 1
        factor = jnp.where(at_row == at_col, cos, jnp.where(at_row == 1, -sin, sin))
        table = factor if table is None else table * factor
    return table


def mix(parts, tan):
    parts = list(parts)
    step = 1
    while step < len(parts):
        for i in range(len(parts)):
            if not i & step:
                u, v = parts[i], parts[i + step]
                parts[i], parts[i + step] = u - tan * v, v + tan * u
        step *= 2
    return parts


def dot(a, b):
    return lax.dot_general(
        a, b, (((1,), (0,)), ((), ())), precision=lax.Precision.HIGHEST, preferred_element_type=F32
    )


def spread(value, shape=(SUB, 128)):
    return jnp.full(shape, value, F32)


def within(parts, lane_table, row_table, tan):
    out = []
    for blocks in parts:
        done = [dot(row_table, dot(block, lane_table)) for block in blocks]
        out.append(mix(done, tan))
    return out


def tables(mix_ref, layer):
    cos0, sin0 = cos_sin(spread(mix_ref[layer, 0], (128, 128)))
    cos1, sin1 = cos_sin(spread(mix_ref[layer, 1], (128, 128)))
    cos2, sin2 = cos_sin(spread(mix_ref[layer, 2], (128, 128)))
    lane_table = plane_table(cos0, sin0, False)
    row_table = plane_table(cos1, sin1, True) * (cos2 * cos2)
    return lane_table, row_table, sin2 / cos2


def first_kernel(mix_ref, wave_ref, level_ref, phase_ref, out_ref):
    lane_table, row_table, tan = tables(mix_ref, 0)
    angle = phase_ref[0:1, :]
    re, im = [], []
    for b in range(4):
        level = level_ref[b]
        cos, sin = cos_sin(level * angle)
        u, v = wave_ref[0, b], wave_ref[1, b]
        re.append(u * cos + v * sin)
        im.append(v * cos - u * sin)
        out_ref[b * 16 : b * 16 + 16, 2] = level.reshape(16, SUB, 128)
    for part, blocks in enumerate(within((re, im), lane_table, row_table, tan)):
        for b in range(4):
            out_ref[b * 16 : b * 16 + 16, part] = blocks[b].reshape(16, SUB, 128)


def middle_kernel(mix_ref, phase_ref, in_ref, out_ref, work_ref):
    scale, tans = None, []
    for layer in range(2):
        cos2, sin2 = cos_sin(spread(mix_ref[layer, 2]))
        cos3, sin3 = cos_sin(spread(mix_ref[layer, 3]))
        tans.append((sin2 / cos2, sin3 / cos3))
        cut = cos2 * cos2 * (cos3 * cos3) * (cos3 * cos3)
        scale = cut if scale is None else scale * cut
    angle = jnp.broadcast_to(phase_ref[1:2, :], (SUB, 128))
    for part in range(2):
        for bank in range(4):
            done = mix([in_ref[bank * 16 + i, part] for i in range(16)], tans[0][1])
            for i in range(16):
                work_ref[bank * 16 + i, part] = done[i]
    for i in range(16):
        re = mix([work_ref[bank * 16 + i, 0] for bank in range(4)], tans[0][0])
        im = mix([work_ref[bank * 16 + i, 1] for bank in range(4)], tans[0][0])
        for bank in range(4):
            cos, sin = cos_sin(in_ref[bank * 16 + i, 2] * angle)
            cos, sin = cos * scale, sin * scale
            u, v = re[bank], im[bank]
            re[bank], im[bank] = u * cos + v * sin, v * cos - u * sin
        re, im = mix(re, tans[1][0]), mix(im, tans[1][0])
        for bank in range(4):
            work_ref[bank * 16 + i, 0] = re[bank]
            work_ref[bank * 16 + i, 1] = im[bank]
    for part in range(2):
        for bank in range(4):
            done = mix([work_ref[bank * 16 + i, part] for i in range(16)], tans[1][1])
            for i in range(16):
                out_ref[bank * 16 + i, part] = done[i]


def last_kernel(mix_ref, in_ref, out_ref):
    lane_table, row_table, tan = tables(mix_ref, 1)
    parts = [[in_ref[b * 16 : b * 16 + 16, part].reshape(128, 128) for b in range(4)] for part in range(2)]
    for part, blocks in enumerate(within(parts, lane_table, row_table, tan)):
        for b in range(4):
            out_ref[part, b] = blocks[b]


VMEM = pl.BlockSpec(memory_space=pltpu.VMEM)
SMEM = pl.BlockSpec(memory_space=pltpu.SMEM)


def swap(values):
    return lax.all_to_all(values, ("bank", "lane"), split_axis=0, concat_axis=0, tiled=True)


def local(wave_parts, level_table, phase_angles, mix_angles):
    send = pl.pallas_call(
        first_kernel,
        out_shape=jax.ShapeDtypeStruct((64, 3, SUB, 128), F32),
        in_specs=[SMEM, VMEM, VMEM, VMEM],
        out_specs=VMEM,
        name="first",
    )(mix_angles, wave_parts, level_table, phase_angles)
    held = swap(send)
    back = pl.pallas_call(
        middle_kernel,
        out_shape=jax.ShapeDtypeStruct((64, 2, SUB, 128), F32),
        in_specs=[SMEM, VMEM, VMEM],
        out_specs=VMEM,
        scratch_shapes=[pltpu.VMEM((64, 2, SUB, 128), F32)],
        name="middle",
    )(mix_angles, phase_angles, held)
    mine = swap(back)
    return pl.pallas_call(
        last_kernel,
        out_shape=jax.ShapeDtypeStruct((2, 4, 128, 128), F32),
        in_specs=[SMEM, VMEM],
        out_specs=VMEM,
        name="last",
    )(mix_angles, mine)


def solution(mesh):
    placed = (
        P("site", ("bank", "lane"), None, None),
        P(("site", "bank", "lane"), None, None),
        P("site", None),
        P("site", None),
    )
    return jax.shard_map(
        local,
        mesh=mesh,
        in_specs=placed,
        out_specs=P("site", ("bank", "lane"), None, None),
        check_vma=False,
    )
```

time: 194 us -> 78.3 us (0.40)
  waiting for transfers between devices: 67.4 us -> 0 us
  starting transfers between devices: 38.1 us -> 0 us
  blocking collectives: 56.3 us -> 68.5 us
  between operations: 11.7 us -> 0.01 us
  local copies, waits for them, and re-layouts: 10.1 us -> 0 us
  Pallas kernels: 0 us -> 9.46 us
  matrix products: 6.27 us -> 0 us
  other arithmetic: 3.22 us -> 0 us
    all_to_all x5 -> x0, waiting for transfers between devices: 67.4 us -> none  [the longest x2 31.6 us: local(): lax.all_to_all(values, 'lane', split_axis=3, concat_axis=1, tiled=True)]
    all_to_all x5 -> x0, starting transfers between devices: 38.1 us -> none  [the longest x2 20.3 us: local(): lax.all_to_all(values, 'lane', split_axis=3, concat_axis=1, tiled=True)]
    all_to_all x3 -> x2, blocking collectives: 56.3 us -> 68.5 us  [swap(): lax.all_to_all(values, ('bank', 'lane'), split_axis=0, concat_axis=0, til...]
    pallas_call x0 -> x3, Pallas kernels: none -> 9.46 us  [the longest x1 3.53 us: local(): pl.pallas_call(first_kernel, out_shape=jax.ShapeDtypeStruct((64, 3, SUB,...]
    dot_general x8 -> x0, matrix products: 6.27 us -> none  [apply_along(): jnp.tensordot(values, real_part, axes=([dim], [0]), precision=lax.Precisi...]
    all_to_all x11 -> x0, local copies, waits for them, and re-layouts: 4.01 us -> none  [the longest x4 2.06 us: local(): lax.all_to_all(moved, 'bank', split_axis=1, concat_axis=2, tiled=True)]
    another operation x2 -> x0, other arithmetic: 3.02 us -> none  [turn_phase(): jnp.stack([values[0] * jnp.cos(turn) + values[1] * jnp.sin(turn), values[...]
    transpose x6 -> x0, local copies, waits for them, and re-layouts: 2.66 us -> none  [apply_along(): return jnp.moveaxis(moved, -1, dim)]
  transfers between devices with their start and end apart: 5 -> 0, of which waited for: 5 -> 0; matrix products, arithmetic and copies ran while one was open for 0% -> 0% of each run, Pallas kernels for 0% -> 0%
where the time goes in v1:
time: 78.3 us; the launch traced here: 78 us
  blocking collectives  68.5 us (87%)
  Pallas kernels  9.46 us (12%)
    all_to_all x2, blocking collectives, swap(): lax.all_to_all(values, ('bank', 'lane'), split_axis=0, concat_axis=0, til...  68.5 us
    pallas_call x1, Pallas kernels, local(): pl.pallas_call(first_kernel, out_shape=jax.ShapeDtypeStruct((64, 3, SUB,...  3.53 us
    pallas_call x1, Pallas kernels, local(): pl.pallas_call(last_kernel, out_shape=jax.ShapeDtypeStruct((2, 4, 128, 12...  3.25 us
    pallas_call x1, Pallas kernels, local(): pl.pallas_call(middle_kernel, out_shape=jax.ShapeDtypeStruct((64, 2, SUB,...  2.69 us

profile of v1, /device:TPU:1, one launch (start us, length us, event | category | flops | bytes accessed | tf_op | source)
XLA Modules:
  0.0 78.0 jit_solution(4025941861309393630)
XLA Ops:
  0.0 3.5 %first.1 = f32[64,3,8,128]{3,2,1,0:T(8,128)} custom-call(f32[2,4]{1,0:T(2,128)} %mix_ref.5, f32[2,4,128,128]{3,2,1,0:T(8,128)} %wave_ref.1, f32[4,128,128]{2,1,0:T(8,128)} %level_ref.1, f32[2,128]{1,0:T(2,128)} %phase_ref.3), custom_call_target="tpu_custom_call" | custom-call | tf_op jit(solution)/shard_map/first/pallas_call | solution.py:147
  3.5 42.1 %all_to_all.10.in_ref = f32[64,3,8,128]{3,2,1,0:T(8,128)} all-to-all(f32[64,3,8,128]{3,2,1,0:T(8,128)} %first.1), channel_id=1, replica_groups=mesh['bank'=4,'lane'=16,'site'=8] {'bank','lane'}, dimensions={0} | all-to-all | bytes 1572864 | tf_op jit(solution)/shard_map/all_to_all | solution.py:143
  45.6 2.7 %middle.1 = f32[64,2,8,128]{3,2,1,0:T(8,128)} custom-call(f32[2,4]{1,0:T(2,128)} %mix_ref.5, f32[2,128]{1,0:T(2,128)} %phase_ref.3, f32[64,3,8,128]{3,2,1,0:T(8,128)} %all_to_all.10.in_ref), custom_call_target="tpu_custom_call" | custom-call | tf_op jit(solution)/shard_map/middle/pallas_call | solution.py:155
  48.3 26.5 %all_to_all.11.in_ref = f32[64,2,8,128]{3,2,1,0:T(8,128)} all-to-all(f32[64,2,8,128]{3,2,1,0:T(8,128)} %middle.1), channel_id=1, replica_groups=mesh['bank'=4,'lane'=16,'site'=8] {'bank','lane'}, dimensions={0} | all-to-all | bytes 1048576 | tf_op jit(solution)/shard_map/all_to_all | solution.py:143
  74.7 3.2 %last.1 = f32[2,4,128,128]{3,2,1,0:T(8,128)} custom-call(f32[2,4]{1,0:T(2,128)} %mix_ref.5, f32[64,2,8,128]{3,2,1,0:T(8,128)} %all_to_all.11.in_ref), custom_call_target="tpu_custom_call" | custom-call | tf_op jit(solution)/shard_map/last/pallas_call | solution.py:164

commit v2 on v1

v2 whole, which is shorter than its diff:
```python
import jax
import jax.numpy as jnp
from jax import lax
from jax.experimental import pallas as pl
from jax.experimental.pallas import tpu as pltpu
from jax.sharding import PartitionSpec as P

SUB = 8
F32 = jnp.float32
BF16 = jnp.bfloat16

SIN = (0.9999999814442071, -0.16666657755521955, 0.008333210982283118, -0.00019834058585468524,
       2.734996203799263e-06, -2.21633008243829e-08)
COS = (0.9999999997000049, -0.4999999949621528, 0.04166665285119409, -0.0013888746708823352,
       2.4794608537121183e-05, -2.7380880775339007e-07, 1.8645524434398867e-09)


def series(z, terms):
    total = z * terms[-1] + terms[-2]
    for term in terms[-3::-1]:
        total = total * z + term
    return total


def cos_sin(x):
    z = x * x
    return series(z, COS), series(z, SIN) * x


def plane_table(cos, sin):
    row = lax.broadcasted_iota(jnp.int32, (128, 128), 0)
    col = lax.broadcasted_iota(jnp.int32, (128, 128), 1)
    apart = row ^ col
    table = None
    for bit in range(7):
        turned = jnp.where((row >> bit) & 1 == 1, -sin, sin)
        factor = jnp.where((apart >> bit) & 1 == 0, cos, turned)
        table = factor if table is None else table * factor
    return table


def halves(x):
    high = x.astype(BF16)
    return high, (x - high.astype(F32)).astype(BF16)


def dot(a, b):
    return lax.dot_general(a, b, (((1,), (0,)), ((), ())), preferred_element_type=F32)


def lane_weights(table):
    high, low = halves(table)
    both = jnp.concatenate([high, low], axis=1)
    return jnp.concatenate([both, both], axis=0)


def row_weights(table):
    high, low = halves(table)
    return jnp.concatenate(
        [jnp.concatenate([high, high], axis=1), jnp.concatenate([low, low], axis=1)], axis=0
    )


def along_lanes(x, weights):
    done = dot(jnp.concatenate(halves(x), axis=1), weights)
    return done[:, :128] + done[:, 128:]


def along_rows(x, weights):
    done = dot(weights, jnp.concatenate(halves(x), axis=0))
    return done[:128] + done[128:]


def mix(parts, tan):
    parts = list(parts)
    step = 1
    while step < len(parts):
        for i in range(len(parts)):
            if not i & step:
                u, v = parts[i], parts[i + step]
                parts[i], parts[i + step] = u - tan * v, v + tan * u
        step *= 2
    return parts


PHASE, TAN2, TAN3, NEXT2, NEXT3, SCALE, COS0, SIN0, COS1, SIN1, TILES = range(11)


def wide(tile):
    return jnp.broadcast_to(tile[0:1], (128, 128))


def first_kernel(mix_hbm, phase_hbm, wave_hbm, level_hbm, out_ref, aux_ref, mix_ref, phase_ref, wave_ref, done_ref, sems):
    small = [
        pltpu.make_async_copy(mix_hbm, mix_ref, sems.at[0]),
        pltpu.make_async_copy(phase_hbm, phase_ref, sems.at[1]),
    ]
    loads = []
    for copy in small:
        copy.start()
    for b in range(4):
        rows = pl.ds(b * 16, 16)
        pair = [
            pltpu.make_async_copy(level_hbm.at[b], out_ref.at[rows, 2], sems.at[2 + 2 * b]),
            pltpu.make_async_copy(wave_hbm.at[:, b], wave_ref.at[:, b], sems.at[3 + 2 * b]),
        ]
        for copy in pair:
            copy.start()
        loads.append(pair)
    for copy in small:
        copy.wait()
    trig = {}
    for layer in range(2):
        for group in range(4):
            angle = jnp.broadcast_to(mix_ref[layer : layer + 1, group : group + 1], (SUB, 128))
            trig[layer, group] = cos_sin(angle)
    tans = {key: sin / cos for key, (cos, sin) in trig.items() if key[1] > 1}
    scale = None
    for layer in range(2):
        cos2, cos3 = trig[layer, 2][0], trig[layer, 3][0]
        cut = cos2 * cos2 * (cos3 * cos3) * (cos3 * cos3)
        scale = cut if scale is None else scale * cut
    scale = scale * trig[0, 2][0] * trig[0, 2][0] * (trig[1, 2][0] * trig[1, 2][0])
    aux_ref[PHASE] = jnp.broadcast_to(phase_ref[1:2, :], (SUB, 128))
    aux_ref[TAN2], aux_ref[TAN3] = tans[0, 2], tans[0, 3]
    aux_ref[NEXT2], aux_ref[NEXT3] = tans[1, 2], tans[1, 3]
    aux_ref[SCALE] = scale
    aux_ref[COS0], aux_ref[SIN0] = trig[1, 0]
    aux_ref[COS1], aux_ref[SIN1] = trig[1, 1]
    lanes = lane_weights(plane_table(wide(trig[0, 0][0]), wide(trig[0, 0][1])))
    rows = row_weights(plane_table(wide(trig[0, 1][0]), wide(-trig[0, 1][1])))
    angle = phase_ref[0:1, :]
    for b in range(4):
        for copy in loads[b]:
            copy.wait()
        cos, sin = cos_sin(out_ref[b * 16 : b * 16 + 16, 2].reshape(128, 128) * angle)
        u, v = wave_ref[0, b].reshape(128, 128), wave_ref[1, b].reshape(128, 128)
        both = jnp.concatenate([u * cos + v * sin, v * cos - u * sin], axis=1)
        both = along_rows(both, rows)
        for part in range(2):
            x = along_lanes(both[:, part * 128 : part * 128 + 128], lanes)
            done_ref[part, b] = x.reshape(16, SUB, 128)
    tan = tans[0, 2]
    for part in range(2):
        for i in range(16):
            out = mix([done_ref[part, b, i] for b in range(4)], tan)
            for b in range(4):
                out_ref[b * 16 + i, part] = out[b]


def middle_kernel(aux_ref, in_ref, out_ref, work_ref):
    angle, scale = aux_ref[PHASE], aux_ref[SCALE]
    tan2, tan3, next2, next3 = aux_ref[TAN2], aux_ref[TAN3], aux_ref[NEXT2], aux_ref[NEXT3]
    for part in range(2):
        for bank in range(4):
            done = mix([in_ref[bank * 16 + i, part] for i in range(16)], tan3)
            for i in range(16):
                work_ref[bank * 16 + i, part] = done[i]
    for i in range(16):
        re = mix([work_ref[bank * 16 + i, 0] for bank in range(4)], tan2)
        im = mix([work_ref[bank * 16 + i, 1] for bank in range(4)], tan2)
        for bank in range(4):
            cos, sin = cos_sin(in_ref[bank * 16 + i, 2] * angle)
            cos, sin = cos * scale, sin * scale
            u, v = re[bank], im[bank]
            re[bank], im[bank] = u * cos + v * sin, v * cos - u * sin
        re, im = mix(re, next2), mix(im, next2)
        for bank in range(4):
            work_ref[bank * 16 + i, 0] = re[bank]
            work_ref[bank * 16 + i, 1] = im[bank]
    for part in range(2):
        for bank in range(4):
            done = mix([work_ref[bank * 16 + i, part] for i in range(16)], next3)
            for i in range(16):
                out_ref[bank * 16 + i, part] = done[i]


def last_kernel(aux_ref, in_ref, out_hbm, work_ref, out_ref, sems):
    tan = aux_ref[NEXT2]
    lanes = lane_weights(plane_table(wide(aux_ref[COS0]), wide(aux_ref[SIN0])))
    rows = row_weights(plane_table(wide(aux_ref[COS1]), wide(-aux_ref[SIN1])))
    for part in range(2):
        for i in range(16):
            out = mix([in_ref[b * 16 + i, part] for b in range(4)], tan)
            for b in range(4):
                work_ref[part, b, i] = out[b]
    copies = []
    for b in range(4):
        both = jnp.concatenate([work_ref[part, b].reshape(128, 128) for part in range(2)], axis=1)
        both = along_rows(both, rows)
        for part in range(2):
            out_ref[part, b] = along_lanes(both[:, part * 128 : part * 128 + 128], lanes)
        copy = pltpu.make_async_copy(out_ref.at[:, b], out_hbm.at[:, b], sems.at[b])
        copy.start()
        copies.append(copy)
    for copy in copies:
        copy.wait()


VMEM = pl.BlockSpec(memory_space=pltpu.VMEM)
HBM = pl.BlockSpec(memory_space=pltpu.HBM)
ROOM = pltpu.CompilerParams(vmem_limit_bytes=12 << 20)


def swap(values):
    return lax.all_to_all(values, ("bank", "lane"), split_axis=0, concat_axis=0, tiled=True)


def local(wave_parts, level_table, phase_angles, mix_angles):
    send, aux = pl.pallas_call(
        first_kernel,
        out_shape=(
            jax.ShapeDtypeStruct((64, 3, SUB, 128), F32),
            jax.ShapeDtypeStruct((TILES, SUB, 128), F32),
        ),
        in_specs=[HBM] * 4,
        out_specs=(VMEM, VMEM),
        scratch_shapes=[
            pltpu.VMEM((2, 4), F32),
            pltpu.VMEM((2, 128), F32),
            pltpu.VMEM((2, 4, 16, SUB, 128), F32),
            pltpu.VMEM((2, 4, 16, SUB, 128), F32),
            pltpu.SemaphoreType.DMA((10,)),
        ],
        compiler_params=ROOM,
        name="first",
    )(*(pltpu.with_memory_space_constraint(v, pltpu.HBM) for v in (mix_angles, phase_angles, wave_parts.reshape(2, 4, 16, SUB, 128), level_table.reshape(4, 16, SUB, 128))))
    held = swap(send)
    back = pl.pallas_call(
        middle_kernel,
        out_shape=jax.ShapeDtypeStruct((64, 2, SUB, 128), F32),
        in_specs=[VMEM, VMEM],
        out_specs=VMEM,
        scratch_shapes=[pltpu.VMEM((64, 2, SUB, 128), F32)],
        compiler_params=ROOM,
        name="middle",
    )(aux, held)
    mine = swap(back)
    return pl.pallas_call(
        last_kernel,
        out_shape=jax.ShapeDtypeStruct((2, 4, 128, 128), F32),
        in_specs=[VMEM, VMEM],
        out_specs=HBM,
        scratch_shapes=[
            pltpu.VMEM((2, 4, 16, SUB, 128), F32),
            pltpu.VMEM((2, 4, 128, 128), F32),
            pltpu.SemaphoreType.DMA((4,)),
        ],
        compiler_params=ROOM,
        name="last",
    )(aux, mine)


def solution(mesh):
    placed = (
        P("site", ("bank", "lane"), None, None),
        P(("site", "bank", "lane"), None, None),
        P("site", None),
        P("site", None),
    )
    return jax.shard_map(
        local,
        mesh=mesh,
        in_specs=placed,
        out_specs=P("site", ("bank", "lane"), None, None),
        check_vma=False,
    )
```

time: 78.3 us -> 73.2 us (0.935)
  Pallas kernels: 9.46 us -> 5.1 us
    pallas_call x1, Pallas kernels: 2.69 us -> 0.72 us  [local(): pl.pallas_call(middle_kernel, out_shape=jax.ShapeDtypeStruct((64, 2, SUB,...]
    pallas_call x1, Pallas kernels: 3.25 us -> 1.48 us  [local(): pl.pallas_call(last_kernel, out_shape=jax.ShapeDtypeStruct((2, 4, 128, 12...]
where the time goes in v2:
time: 73.2 us; the launch traced here: 73 us
  blocking collectives  67.9 us (93%)
  Pallas kernels  5.1 us (7%)
    all_to_all x2, blocking collectives, swap(): lax.all_to_all(values, ('bank', 'lane'), split_axis=0, concat_axis=0, til...  67.9 us
    pallas_call x1, Pallas kernels, local(): pl.pallas_call(first_kernel, out_shape=(jax.ShapeDtypeStruct((64, 3, SUB,...  2.9 us
    pallas_call x1, Pallas kernels, local(): pl.pallas_call(last_kernel, out_shape=jax.ShapeDtypeStruct((2, 4, 128, 12...  1.48 us

profile of v2, /device:TPU:1, one launch (start us, length us, event | category | flops | bytes accessed | tf_op | source)
XLA Modules:
  0.0 73.0 jit_solution(4737617724098764159)
XLA Ops:
  0.0 2.9 %first.1 = (f32[64,3,8,128]{3,2,1,0:T(8,128)S(1)}, f32[10,8,128]{2,1,0:T(8,128)S(1)}) custom-call(f32[2,4]{1,0:T(2,128)} %mix_hbm.1, f32[2,128]{1,0:T(2,128)} %phase_hbm.1, f32[2,4,16,8,128]{4,3,2,1,0:T(8,128)} %bitcast.2, f32[4,16,8,128]{3,2,1,0:T(8,128)} %bitcast.3), custom_call_target="tpu_custom_call" | custom-call | tf_op jit(solution)/shard_map/first/pallas_call | solution.py:210
  2.9 41.7 %all_to_all.10.in_ref = f32[64,3,8,128]{3,2,1,0:T(8,128)S(1)} all-to-all(f32[64,3,8,128]{3,2,1,0:T(8,128)S(1)} %get-tuple-element.8), channel_id=1, replica_groups=mesh['bank'=4,'lane'=16,'site'=8] {'bank','lane'}, dimensions={0} | all-to-all | bytes 1572864 | tf_op jit(solution)/shard_map/all_to_all | solution.py:206
  44.7 0.7 middle.1
  45.4 26.2 %all_to_all.11.in_ref = f32[64,2,8,128]{3,2,1,0:T(8,128)S(1)} all-to-all(f32[64,2,8,128]{3,2,1,0:T(8,128)S(1)} %middle.1), channel_id=1, replica_groups=mesh['bank'=4,'lane'=16,'site'=8] {'bank','lane'}, dimensions={0} | all-to-all | bytes 1048576 | tf_op jit(solution)/shard_map/all_to_all | solution.py:206
  71.6 1.5 %last.1 = f32[2,4,128,128]{3,2,1,0:T(8,128)} custom-call(f32[10,8,128]{2,1,0:T(8,128)S(1)} %get-tuple-element.7.aux_ref, f32[64,2,8,128]{3,2,1,0:T(8,128)S(1)} %all_to_all.11.in_ref), custom_call_target="tpu_custom_call" | custom-call | tf_op jit(solution)/shard_map/last/pallas_call | solution.py:239

commit v3 on v2

--- a/solution.py
+++ b/solution.py
@@ -6,6 +6,13 @@
 from jax.sharding import PartitionSpec as P
 
 SUB = 8
+ORDER = [
+    (bank + 2) % 4 * 16 + (y + 4) % 8 * 2 + 1 - core
+    for y in range(8)
+    for core in range(2)
+    for bank in range(4)
+]
+PLACE = [ORDER.index(k) for k in range(64)]
 F32 = jnp.float32
 BF16 = jnp.bfloat16
 
@@ -130,15 +137,17 @@
     lanes = lane_weights(plane_table(wide(trig[0, 0][0]), wide(trig[0, 0][1])))
     rows = row_weights(plane_table(wide(trig[0, 1][0]), wide(-trig[0, 1][1])))
     angle = phase_ref[0:1, :]
+    for pair in loads:
+        for copy in pair:
+            copy.wait()
     for b in range(4):
-        for copy in loads[b]:
-            copy.wait()
         cos, sin = cos_sin(out_ref[b * 16 : b * 16 + 16, 2].reshape(128, 128) * angle)
         u, v = wave_ref[0, b].reshape(128, 128), wave_ref[1, b].reshape(128, 128)
         both = jnp.concatenate([u * cos + v * sin, v * cos - u * sin], axis=1)
         both = along_rows(both, rows)
         for part in range(2):
-            x = along_lanes(both[:, part * 128 : part * 128 + 128], lanes)
+            x = both[:, part * 128 : part * 128 + 128]
+            x = along_lanes(x, lanes)
             done_ref[part, b] = x.reshape(16, SUB, 128)
     tan = tans[0, 2]
     for part in range(2):
@@ -153,14 +162,14 @@
     tan2, tan3, next2, next3 = aux_ref[TAN2], aux_ref[TAN3], aux_ref[NEXT2], aux_ref[NEXT3]
     for part in range(2):
         for bank in range(4):
-            done = mix([in_ref[bank * 16 + i, part] for i in range(16)], tan3)
+            done = mix([in_ref[PLACE[bank * 16 + i], part] for i in range(16)], tan3)
             for i in range(16):
                 work_ref[bank * 16 + i, part] = done[i]
     for i in range(16):
         re = mix([work_ref[bank * 16 + i, 0] for bank in range(4)], tan2)
         im = mix([work_ref[bank * 16 + i, 1] for bank in range(4)], tan2)
         for bank in range(4):
-            cos, sin = cos_sin(in_ref[bank * 16 + i, 2] * angle)
+            cos, sin = cos_sin(in_ref[PLACE[bank * 16 + i], 2] * angle)
             cos, sin = cos * scale, sin * scale
             u, v = re[bank], im[bank]
             re[bank], im[bank] = u * cos + v * sin, v * cos - u * sin
@@ -172,7 +181,7 @@
         for bank in range(4):
             done = mix([work_ref[bank * 16 + i, part] for i in range(16)], next3)
             for i in range(16):
-                out_ref[bank * 16 + i, part] = done[i]
+                out_ref[PLACE[bank * 16 + i], part] = done[i]
 
 
 def last_kernel(aux_ref, in_ref, out_hbm, work_ref, out_ref, sems):
@@ -203,7 +212,9 @@
 
 
 def swap(values):
-    return lax.all_to_all(values, ("bank", "lane"), split_axis=0, concat_axis=0, tiled=True)
+    return lax.all_to_all(
+        values, ("bank", "lane"), split_axis=0, concat_axis=0, axis_index_groups=[ORDER], tiled=True
+    )
 
 
 def local(wave_parts, level_table, phase_angles, mix_angles):

time: 73.2 us -> 66.7 us (0.911)
  blocking collectives: 67.9 us -> 62.3 us
  Pallas kernels: 5.1 us -> 4.25 us
    all_to_all x2, blocking collectives: 67.9 us -> 62.3 us  [swap(): lax.all_to_all(values, ('bank', 'lane'), split_axis=0, concat_axis=0, axi...]
    pallas_call x1, Pallas kernels: 2.9 us -> 2.03 us  [local(): pl.pallas_call(first_kernel, out_shape=(jax.ShapeDtypeStruct((64, 3, SUB,...]
where the time goes in v3:
time: 66.7 us; the launch traced here: 66.5 us
  blocking collectives  62.3 us (93%)
  Pallas kernels  4.25 us (6%)
    all_to_all x2, blocking collectives, swap(): lax.all_to_all(values, ('bank', 'lane'), split_axis=0, concat_axis=0, axi...  62.3 us
    pallas_call x1, Pallas kernels, local(): pl.pallas_call(first_kernel, out_shape=(jax.ShapeDtypeStruct((64, 3, SUB,...  2.03 us
    pallas_call x1, Pallas kernels, local(): pl.pallas_call(last_kernel, out_shape=jax.ShapeDtypeStruct((2, 4, 128, 12...  1.48 us

profile of v3, /device:TPU:1, one launch (start us, length us, event | category | flops | bytes accessed | tf_op | source)
XLA Modules:
  0.0 66.5 jit_solution(2984053158889705028)
XLA Ops:
  0.0 2.0 %first.1 = (f32[64,3,8,128]{3,2,1,0:T(8,128)S(1)}, f32[10,8,128]{2,1,0:T(8,128)S(1)}) custom-call(f32[2,4]{1,0:T(2,128)} %mix_hbm.1, f32[2,128]{1,0:T(2,128)} %phase_hbm.1, f32[2,4,16,8,128]{4,3,2,1,0:T(8,128)} %bitcast.2, f32[4,16,8,128]{3,2,1,0:T(8,128)} %bitcast.3), custom_call_target="tpu_custom_call" | custom-call | tf_op jit(solution)/shard_map/first/pallas_call | solution.py:221
  2.0 37.2 %all_to_all.10.in_ref = f32[64,3,8,128]{3,2,1,0:T(8,128)S(1)} all-to-all(f32[64,3,8,128]{3,2,1,0:T(8,128)S(1)} %get-tuple-element.8), channel_id=1, replica_groups={{328,456,72,200,320,448,64,192,344,472,88,216,336,464,80,208,360,488,10..., dimensions={0} | all-to-all | bytes 1572864 | tf_op jit(solution)/shard_map/all_to_all | solution.py:215
  39.2 0.7 %middle.1 = f32[64,2,8,128]{3,2,1,0:T(8,128)S(1)} custom-call(f32[10,8,128]{2,1,0:T(8,128)S(1)} %get-tuple-element.7.aux_ref, f32[64,3,8,128]{3,2,1,0:T(8,128)S(1)} %all_to_all.10.in_ref), custom_call_target="tpu_custom_call" | custom-call | tf_op jit(solution)/shard_map/middle/pallas_call | solution.py:240
  40.0 25.1 %all_to_all.11.in_ref = f32[64,2,8,128]{3,2,1,0:T(8,128)S(1)} all-to-all(f32[64,2,8,128]{3,2,1,0:T(8,128)S(1)} %middle.1), channel_id=1, replica_groups={{328,456,72,200,320,448,64,192,344,472,88,216,336,464,80,208,360,488,10..., dimensions={0} | all-to-all | bytes 1048576 | tf_op jit(solution)/shard_map/all_to_all | solution.py:215
  65.1 1.5 %last.1 = f32[2,4,128,128]{3,2,1,0:T(8,128)} custom-call(f32[10,8,128]{2,1,0:T(8,128)S(1)} %get-tuple-element.7.aux_ref, f32[64,2,8,128]{3,2,1,0:T(8,128)S(1)} %all_to_all.11.in_ref), custom_call_target="tpu_custom_call" | custom-call | tf_op jit(solution)/shard_map/last/pallas_call | solution.py:250

commit v4 on v3

v4 whole, which is shorter than its diff:
```python
import jax
import jax.numpy as jnp
from jax import lax
from jax.experimental import pallas as pl
from jax.experimental.pallas import tpu as pltpu
from jax.sharding import PartitionSpec as P

SUB = 8
ORDER = [
    bank * 16 + (y + 4) % 8 * 2 + 1 - core for y in range(8) for core in range(2) for bank in (2, 0, 3, 1)
]
PLACE = [ORDER.index(k) for k in range(64)]
F32 = jnp.float32
BF16 = jnp.bfloat16

SIN = (0.9999999814442071, -0.16666657755521955, 0.008333210982283118, -0.00019834058585468524,
       2.734996203799263e-06, -2.21633008243829e-08)
COS = (0.9999999997000049, -0.4999999949621528, 0.04166665285119409, -0.0013888746708823352,
       2.4794608537121183e-05, -2.7380880775339007e-07, 1.8645524434398867e-09)


def series(z, terms):
    total = z * terms[-1] + terms[-2]
    for term in terms[-3::-1]:
        total = total * z + term
    return total


def cos_sin(x):
    z = x * x
    return series(z, COS), series(z, SIN) * x


def plane_table(cos, sin, bits):
    row = lax.broadcasted_iota(jnp.int32, (128, 128), 0)
    col = lax.broadcasted_iota(jnp.int32, (128, 128), 1)
    apart = row ^ col
    table = jnp.where(apart >> bits == 0, 1.0, 0.0).astype(F32)
    for bit in range(bits):
        turned = jnp.where((row >> bit) & 1 == 1, -sin, sin)
        table = table * jnp.where((apart >> bit) & 1 == 0, cos, turned)
    return table


def halves(x):
    high = x.astype(BF16)
    return high, (x - high.astype(F32)).astype(BF16)


def dot(a, b):
    return lax.dot_general(a, b, (((1,), (0,)), ((), ())), preferred_element_type=F32)


def lane_weights(table):
    both = jnp.concatenate(halves(table), axis=1)
    return jnp.concatenate([both, both], axis=0)


def row_weights(table):
    return jnp.concatenate([jnp.concatenate([half, half], axis=1) for half in halves(table)], axis=0)


def within(parts, lanes, rows):
    both = jnp.concatenate([jnp.concatenate(tiles, axis=0) for tiles in parts], axis=1)
    both = dot(rows, jnp.concatenate(halves(both), axis=0))
    both = both[:128] + both[128:]
    out = []
    for part in range(2):
        done = dot(jnp.concatenate(halves(both[:, part * 128 : part * 128 + 128]), axis=1), lanes)
        done = done[:, :128] + done[:, 128:]
        out.append([done[i * SUB : i * SUB + SUB] for i in range(16)])
    return out


def mix(parts, tan):
    parts = list(parts)
    step = 1
    while step < len(parts):
        for i in range(len(parts)):
            if not i & step:
                u, v = parts[i], parts[i + step]
                parts[i], parts[i + step] = u - tan * v, v + tan * u
        step *= 2
    return parts


PHASE, SCALE, TAN2, TAN3, NEXT1, NEXT2, NEXT3, TILES = range(8)


def wide(tile):
    return jnp.broadcast_to(tile[0:1], (128, 128))


def trig_of(mix_ref, layer, group):
    return cos_sin(jnp.broadcast_to(mix_ref[layer : layer + 1, group : group + 1], (SUB, 128)))


def share(mix_ref, phase_ref, aux_ref, lanes_ref, rows_ref):
    scale, tans = None, {}
    for layer in range(2):
        trig = [trig_of(mix_ref, layer, group) for group in range(4)]
        for group, (cos, sin) in enumerate(trig):
            tans[layer, group] = sin / cos
        cut = trig[1][0] * trig[2][0] * trig[3][0]
        cut = cut * cut
        cut = cut * cut
        scale = cut if scale is None else scale * cut
        lanes_ref[layer] = lane_weights(plane_table(wide(trig[0][0]), wide(trig[0][1]), 7))
        rows_ref[layer] = row_weights(plane_table(wide(trig[1][0]), wide(-trig[1][1]), 3))
    aux_ref[PHASE] = jnp.broadcast_to(phase_ref[1:2, :], (SUB, 128))
    aux_ref[SCALE] = scale
    aux_ref[TAN2], aux_ref[TAN3] = tans[0, 2], tans[0, 3]
    aux_ref[NEXT1], aux_ref[NEXT2], aux_ref[NEXT3] = tans[1, 1], tans[1, 2], tans[1, 3]
    return tans[0, 1], tans[0, 2]


def first_kernel(
    mix_hbm, phase_hbm, wave_hbm, level_hbm, out_ref, aux_ref, lanes_ref, rows_ref, mix_ref, phase_ref, wave_ref, sems
):
    small = [
        pltpu.make_async_copy(mix_hbm, mix_ref, sems.at[0]),
        pltpu.make_async_copy(phase_hbm, phase_ref, sems.at[1]),
    ]
    loads = []
    for copy in small:
        copy.start()
    for b in range(4):
        pair = [
            pltpu.make_async_copy(level_hbm.at[b], out_ref.at[pl.ds(b * 16, 16), 2], sems.at[2 + 2 * b]),
            pltpu.make_async_copy(wave_hbm.at[:, b], wave_ref.at[:, b], sems.at[3 + 2 * b]),
        ]
        for copy in pair:
            copy.start()
        loads.append(pair)
    for copy in small:
        copy.wait()
    tans = share(mix_ref, phase_ref, aux_ref, lanes_ref, rows_ref)
    angle = jnp.broadcast_to(phase_ref[0:1, :], (SUB, 128))
    for b in range(4):
        for copy in loads[b]:
            copy.wait()
        re, im = [], []
        for i in range(16):
            cos, sin = cos_sin(out_ref[b * 16 + i, 2] * angle)
            u, v = wave_ref[0, b, i], wave_ref[1, b, i]
            re.append(u * cos + v * sin)
            im.append(v * cos - u * sin)
        for part, tiles in enumerate((re, im)):
            for i, tile in enumerate(mix(tiles, tans[0])):
                wave_ref[part, b, i] = tile
    for part in range(2):
        for i in range(16):
            for b, tile in enumerate(mix([wave_ref[part, b, i] for b in range(4)], tans[1])):
                out_ref[b * 16 + i, part] = tile


def middle_kernel(aux_ref, lanes_ref, rows_ref, in_ref, out_ref, work_ref):
    angle, scale = aux_ref[PHASE], aux_ref[SCALE]
    tan2, tan3, next2, next3 = aux_ref[TAN2], aux_ref[TAN3], aux_ref[NEXT2], aux_ref[NEXT3]
    lanes, rows = lanes_ref[0], rows_ref[0]
    for bank in range(4):
        parts = [mix([in_ref[PLACE[bank * 16 + i], part] for i in range(16)], tan3) for part in range(2)]
        parts = within(parts, lanes, rows)
        for part in range(2):
            for i in range(16):
                work_ref[bank, i, part] = parts[part][i]
    for i in range(16):
        re = mix([work_ref[bank, i, 0] for bank in range(4)], tan2)
        im = mix([work_ref[bank, i, 1] for bank in range(4)], tan2)
        for bank in range(4):
            cos, sin = cos_sin(in_ref[PLACE[bank * 16 + i], 2] * angle)
            cos, sin = cos * scale, sin * scale
            u, v = re[bank], im[bank]
            re[bank], im[bank] = u * cos + v * sin, v * cos - u * sin
        re, im = mix(re, next2), mix(im, next2)
        for bank in range(4):
            work_ref[bank, i, 0] = re[bank]
            work_ref[bank, i, 1] = im[bank]
    lanes, rows = lanes_ref[1], rows_ref[1]
    for bank in range(4):
        parts = within([[work_ref[bank, i, part] for i in range(16)] for part in range(2)], lanes, rows)
        for part in range(2):
            for i, tile in enumerate(mix(parts[part], next3)):
                out_ref[PLACE[bank * 16 + i], part] = tile


def last_kernel(aux_ref, in_ref, out_hbm, work_ref, out_ref, sems):
    next1, next2 = aux_ref[NEXT1], aux_ref[NEXT2]
    for part in range(2):
        for i in range(16):
            for b, tile in enumerate(mix([in_ref[b * 16 + i, part] for b in range(4)], next2)):
                work_ref[part, b, i] = tile
    copies = []
    for b in range(4):
        for part in range(2):
            for i, tile in enumerate(mix([work_ref[part, b, i] for i in range(16)], next1)):
                out_ref[part, b, i] = tile
        copy = pltpu.make_async_copy(out_ref.at[:, b], out_hbm.at[:, b], sems.at[b])
        copy.start()
        copies.append(copy)
    for copy in copies:
        copy.wait()


VMEM = pl.BlockSpec(memory_space=pltpu.VMEM)
HBM = pl.BlockSpec(memory_space=pltpu.HBM)
ROOM = pltpu.CompilerParams(vmem_limit_bytes=12 << 20)


def swap(values):
    return lax.all_to_all(
        values, ("bank", "lane"), split_axis=0, concat_axis=0, axis_index_groups=[ORDER], tiled=True
    )


def local(wave_parts, level_table, phase_angles, mix_angles):
    wave_parts, level_table, phase_angles, mix_angles = (
        pltpu.with_memory_space_constraint(v, pltpu.HBM)
        for v in (
            wave_parts.reshape(2, 4, 16, SUB, 128),
            level_table.reshape(4, 16, SUB, 128),
            phase_angles,
            mix_angles,
        )
    )
    send, aux, lanes, rows = pl.pallas_call(
        first_kernel,
        out_shape=(
            jax.ShapeDtypeStruct((64, 3, SUB, 128), F32),
            jax.ShapeDtypeStruct((TILES, SUB, 128), F32),
            jax.ShapeDtypeStruct((2, 256, 256), BF16),
            jax.ShapeDtypeStruct((2, 256, 256), BF16),
        ),
        in_specs=[HBM] * 4,
        out_specs=(VMEM,) * 4,
        scratch_shapes=[
            pltpu.VMEM((2, 4), F32),
            pltpu.VMEM((2, 128), F32),
            pltpu.VMEM((2, 4, 16, SUB, 128), F32),
            pltpu.SemaphoreType.DMA((10,)),
        ],
        compiler_params=ROOM,
        name="first",
    )(mix_angles, phase_angles, wave_parts, level_table)
    held = swap(send)
    back = pl.pallas_call(
        middle_kernel,
        out_shape=jax.ShapeDtypeStruct((64, 2, SUB, 128), F32),
        in_specs=[VMEM] * 4,
        out_specs=VMEM,
        scratch_shapes=[pltpu.VMEM((4, 16, 2, SUB, 128), F32)],
        compiler_params=ROOM,
        name="middle",
    )(aux, lanes, rows, held)
    mine = swap(back)
    out = pl.pallas_call(
        last_kernel,
        out_shape=jax.ShapeDtypeStruct((2, 4, 16, SUB, 128), F32),
        in_specs=[VMEM, VMEM],
        out_specs=HBM,
        scratch_shapes=[
            pltpu.VMEM((2, 4, 16, SUB, 128), F32),
            pltpu.VMEM((2, 4, 16, SUB, 128), F32),
            pltpu.SemaphoreType.DMA((4,)),
        ],
        compiler_params=ROOM,
        name="last",
    )(aux, mine)
    return out.reshape(2, 4, 128, 128)


def solution(mesh):
    placed = (
        P("site", ("bank", "lane"), None, None),
        P(("site", "bank", "lane"), None, None),
        P("site", None),
        P("site", None),
    )
    return jax.shard_map(
        local,
        mesh=mesh,
        in_specs=placed,
        out_specs=P("site", ("bank", "lane"), None, None),
        check_vma=False,
    )
```

time: 66.7 us -> 66.6 us (level)
    pallas_call x1, Pallas kernels: 0.74 us -> 1.46 us  [local(): pl.pallas_call(middle_kernel, out_shape=jax.ShapeDtypeStruct((64, 2, SUB,...]
where the time goes in v4:
time: 66.6 us; the launch traced here: 66.4 us
  blocking collectives  62.2 us (93%)
  Pallas kernels  4.15 us (6%)
    all_to_all x2, blocking collectives, swap(): lax.all_to_all(values, ('bank', 'lane'), split_axis=0, concat_axis=0, axi...  62.2 us
    pallas_call x1, Pallas kernels, local(): pl.pallas_call(first_kernel, out_shape=(jax.ShapeDtypeStruct((64, 3, SUB,...  1.78 us
    pallas_call x1, Pallas kernels, local(): pl.pallas_call(middle_kernel, out_shape=jax.ShapeDtypeStruct((64, 2, SUB,...  1.46 us

profile of v4, /device:TPU:1, one launch (start us, length us, event | category | flops | bytes accessed | tf_op | source)
XLA Modules:
  0.0 66.4 jit_solution(13093617266577022780)
XLA Ops:
  0.0 1.8 %first.1 = (f32[64,3,8,128]{3,2,1,0:T(8,128)S(1)}, f32[7,8,128]{2,1,0:T(8,128)S(1)}, bf16[2,256,256]{2,1,0:T(8,128)(2,1)S(1)}, bf16[2,256,256]{2,1,0:T(8,128)(2,1)S(1)}) custom-call(f32[2,4]{1,0:T(2,128)} %mix_hbm.1, f32[2,128]{1,0:T(2,128)} %phase_hbm.1, f32[2,4,16,8,128]{4,3,2,1,0:T(8,128)} %bitcast.3, f32[4,16,8,128]{3,2,1,0:T(8,128)} %bitcast.4), custom_call_target="tpu_custom_call" | custom-call | tf_op jit(solution)/shard_map/first/pallas_call | solution.py:226
  1.8 37.1 %all_to_all.10.in_ref = f32[64,3,8,128]{3,2,1,0:T(8,128)S(1)} all-to-all(f32[64,3,8,128]{3,2,1,0:T(8,128)S(1)} %get-tuple-element.12), channel_id=1, replica_groups={{328,72,456,200,320,64,448,192,344,88,472,216,336,80,464,208,360,104,48..., dimensions={0} | all-to-all | bytes 1572864 | tf_op jit(solution)/shard_map/all_to_all | solution.py:211
  38.9 1.5 %middle.1 = f32[64,2,8,128]{3,2,1,0:T(8,128)S(1)} custom-call(f32[7,8,128]{2,1,0:T(8,128)S(1)} %get-tuple-element.9.aux_ref, bf16[2,256,256]{2,1,0:T(8,128)(2,1)S(1)} %get-tuple-element.10.lanes_ref, bf16[2,256,256]{2,1,0:T(8,128)(2,1)S(1)} %get-tuple-element.11.rows_ref, f32[64,3,8,128]{3,2,1,0:T(8,128)S(1)} %all_to_all.10.in_ref), custom_call_target="tpu_custom_call" | custom-call | tf_op jit(solution)/shard_map/middle/pallas_call | solution.py:246
  40.3 25.1 %all_to_all.11.in_ref = f32[64,2,8,128]{3,2,1,0:T(8,128)S(1)} all-to-all(f32[64,2,8,128]{3,2,1,0:T(8,128)S(1)} %middle.1), channel_id=1, replica_groups={{328,72,456,200,320,64,448,192,344,88,472,216,336,80,464,208,360,104,48..., dimensions={0} | all-to-all | bytes 1048576 | tf_op jit(solution)/shard_map/all_to_all | solution.py:211
  65.5 0.9 %last.1 = f32[2,4,16,8,128]{4,3,2,1,0:T(8,128)} custom-call(f32[7,8,128]{2,1,0:T(8,128)S(1)} %get-tuple-element.9.aux_ref, f32[64,2,8,128]{3,2,1,0:T(8,128)S(1)} %all_to_all.11.in_ref), custom_call_target="tpu_custom_call" | custom-call | tf_op jit(solution)/shard_map/last/pallas_call | solution.py:256

commit v5 on v4

--- a/solution.py
+++ b/solution.py
@@ -31,15 +31,36 @@
     return series(z, COS), series(z, SIN) * x
 
 
-def plane_table(cos, sin, bits):
-    row = lax.broadcasted_iota(jnp.int32, (128, 128), 0)
-    col = lax.broadcasted_iota(jnp.int32, (128, 128), 1)
-    apart = row ^ col
-    table = jnp.where(apart >> bits == 0, 1.0, 0.0).astype(F32)
-    for bit in range(bits):
-        turned = jnp.where((row >> bit) & 1 == 1, -sin, sin)
-        table = table * jnp.where((apart >> bit) & 1 == 0, cos, turned)
-    return table
+def bit_factor(cos, sin, column, bit, row_bit):
+    at = (column >> bit) & 1
+    if isinstance(row_bit, bool):
+        return jnp.where(at == row_bit, cos, -sin if row_bit else sin)
+    return jnp.where(at == row_bit, cos, jnp.where(row_bit == 1, -sin, sin))
+
+
+def low_table(cos, sin):
+    row = lax.broadcasted_iota(jnp.int32, (SUB, 128), 0)
+    column = lax.broadcasted_iota(jnp.int32, (SUB, 128), 1)
+    tile = None
+    for bit in range(3):
+        factor = bit_factor(cos, sin, column, bit, (row >> bit) & 1)
+        tile = factor if tile is None else tile * factor
+    return tile
+
+
+def lane_table(cos, sin):
+    column = lax.broadcasted_iota(jnp.int32, (SUB, 128), 1)
+    tiles = [low_table(cos, sin)]
+    for bit in range(3, 7):
+        pair = [bit_factor(cos, sin, column, bit, at) for at in (False, True)]
+        tiles = [tile * factor for factor in pair for tile in tiles]
+    return jnp.concatenate(tiles, axis=0)
+
+
+def row_table(cos, sin):
+    tile = low_table(cos, -sin)
+    group = lax.broadcasted_iota(jnp.int32, (SUB, 128), 1) >> 3
+    return jnp.concatenate([jnp.where(group == i, tile, 0.0) for i in range(16)], axis=0)
 
 
 def halves(x):
@@ -87,10 +108,6 @@
 PHASE, SCALE, TAN2, TAN3, NEXT1, NEXT2, NEXT3, TILES = range(8)
 
 
-def wide(tile):
-    return jnp.broadcast_to(tile[0:1], (128, 128))
-
-
 def trig_of(mix_ref, layer, group):
     return cos_sin(jnp.broadcast_to(mix_ref[layer : layer + 1, group : group + 1], (SUB, 128)))
 
@@ -105,8 +122,8 @@
         cut = cut * cut
         cut = cut * cut
         scale = cut if scale is None else scale * cut
-        lanes_ref[layer] = lane_weights(plane_table(wide(trig[0][0]), wide(trig[0][1]), 7))
-        rows_ref[layer] = row_weights(plane_table(wide(trig[1][0]), wide(-trig[1][1]), 3))
+        lanes_ref[layer] = lane_weights(lane_table(*trig[0]))
+        rows_ref[layer] = row_weights(row_table(*trig[1]))
     aux_ref[PHASE] = jnp.broadcast_to(phase_ref[1:2, :], (SUB, 128))
     aux_ref[SCALE] = scale
     aux_ref[TAN2], aux_ref[TAN3] = tans[0, 2], tans[0, 3]

time: 66.6 us -> 66.4 us (level)
  no operation moved by 1% of the time
where the time goes in v5:
time: 66.4 us; the launch traced here: 66.2 us
  blocking collectives  62.2 us (94%)
  Pallas kernels  3.93 us (6%)
    all_to_all x2, blocking collectives, swap(): lax.all_to_all(values, ('bank', 'lane'), split_axis=0, concat_axis=0, axi...  62.2 us
    pallas_call x1, Pallas kernels, local(): pl.pallas_call(first_kernel, out_shape=(jax.ShapeDtypeStruct((64, 3, SUB,...  1.56 us
    pallas_call x1, Pallas kernels, local(): pl.pallas_call(middle_kernel, out_shape=jax.ShapeDtypeStruct((64, 2, SUB,...  1.46 us

profile of v5, /device:TPU:1, one launch (start us, length us, event | category | flops | bytes accessed | tf_op | source)
XLA Modules:
  0.0 66.2 jit_solution(5395483049752726418)
XLA Ops:
  0.0 1.6 %first.1 = (f32[64,3,8,128]{3,2,1,0:T(8,128)S(1)}, f32[7,8,128]{2,1,0:T(8,128)S(1)}, bf16[2,256,256]{2,1,0:T(8,128)(2,1)S(1)}, bf16[2,256,256]{2,1,0:T(8,128)(2,1)S(1)}) custom-call(f32[2,4]{1,0:T(2,128)} %mix_hbm.1, f32[2,128]{1,0:T(2,128)} %phase_hbm.1, f32[2,4,16,8,128]{4,3,2,1,0:T(8,128)} %bitcast.3, f32[4,16,8,128]{3,2,1,0:T(8,128)} %bitcast.4), custom_call_target="tpu_custom_call" | custom-call | tf_op jit(solution)/shard_map/first/pallas_call | solution.py:243
  1.6 37.1 %all_to_all.10.in_ref = f32[64,3,8,128]{3,2,1,0:T(8,128)S(1)} all-to-all(f32[64,3,8,128]{3,2,1,0:T(8,128)S(1)} %get-tuple-element.12), channel_id=1, replica_groups={{328,72,456,200,320,64,448,192,344,88,472,216,336,80,464,208,360,104,48..., dimensions={0} | all-to-all | bytes 1572864 | tf_op jit(solution)/shard_map/all_to_all | solution.py:228
  38.6 1.5 %middle.1 = f32[64,2,8,128]{3,2,1,0:T(8,128)S(1)} custom-call(f32[7,8,128]{2,1,0:T(8,128)S(1)} %get-tuple-element.9.aux_ref, bf16[2,256,256]{2,1,0:T(8,128)(2,1)S(1)} %get-tuple-element.10.lanes_ref, bf16[2,256,256]{2,1,0:T(8,128)(2,1)S(1)} %get-tuple-element.11.rows_ref, f32[64,3,8,128]{3,2,1,0:T(8,128)S(1)} %all_to_all.10.in_ref), custom_call_target="tpu_custom_call" | custom-call | tf_op jit(solution)/shard_map/middle/pallas_call | solution.py:263
  40.1 25.2 %all_to_all.11.in_ref = f32[64,2,8,128]{3,2,1,0:T(8,128)S(1)} all-to-all(f32[64,2,8,128]{3,2,1,0:T(8,128)S(1)} %middle.1), channel_id=1, replica_groups={{328,72,456,200,320,64,448,192,344,88,472,216,336,80,464,208,360,104,48..., dimensions={0} | all-to-all | bytes 1048576 | tf_op jit(solution)/shard_map/all_to_all | solution.py:228
  65.3 0.9 %last.1 = f32[2,4,16,8,128]{4,3,2,1,0:T(8,128)} custom-call(f32[7,8,128]{2,1,0:T(8,128)S(1)} %get-tuple-element.9.aux_ref, f32[64,2,8,128]{3,2,1,0:T(8,128)S(1)} %all_to_all.11.in_ref), custom_call_target="tpu_custom_call" | custom-call | tf_op jit(solution)/shard_map/last/pallas_call | solution.py:273

commit v6 on v5

--- a/solution.py
+++ b/solution.py
@@ -48,19 +48,13 @@
     return tile
 
 
-def lane_table(cos, sin):
+def seven_bits(low, high):
     column = lax.broadcasted_iota(jnp.int32, (SUB, 128), 1)
-    tiles = [low_table(cos, sin)]
+    tiles = [low_table(*low)]
     for bit in range(3, 7):
-        pair = [bit_factor(cos, sin, column, bit, at) for at in (False, True)]
+        pair = [bit_factor(*high, column, bit, at) for at in (False, True)]
         tiles = [tile * factor for factor in pair for tile in tiles]
     return jnp.concatenate(tiles, axis=0)
-
-
-def row_table(cos, sin):
-    tile = low_table(cos, -sin)
-    group = lax.broadcasted_iota(jnp.int32, (SUB, 128), 1) >> 3
-    return jnp.concatenate([jnp.where(group == i, tile, 0.0) for i in range(16)], axis=0)
 
 
 def halves(x):
@@ -82,15 +76,14 @@
 
 
 def within(parts, lanes, rows):
+    count = len(parts)
     both = jnp.concatenate([jnp.concatenate(tiles, axis=0) for tiles in parts], axis=1)
     both = dot(rows, jnp.concatenate(halves(both), axis=0))
     both = both[:128] + both[128:]
-    out = []
-    for part in range(2):
-        done = dot(jnp.concatenate(halves(both[:, part * 128 : part * 128 + 128]), axis=1), lanes)
-        done = done[:, :128] + done[:, 128:]
-        out.append([done[i * SUB : i * SUB + SUB] for i in range(16)])
-    return out
+    tall = jnp.concatenate([both[:, i * 128 : i * 128 + 128] for i in range(count)], axis=0)
+    done = dot(jnp.concatenate(halves(tall), axis=1), lanes)
+    done = done[:, :128] + done[:, 128:]
+    return [[done[(j * 16 + i) * SUB : (j * 16 + i + 1) * SUB] for i in range(16)] for j in range(count)]
 
 
 def mix(parts, tan):
@@ -105,7 +98,7 @@
     return parts
 
 
-PHASE, SCALE, TAN2, TAN3, NEXT1, NEXT2, NEXT3, TILES = range(8)
+PHASE, SCALE, TAN2, NEXT1, NEXT2, TILES = range(6)
 
 
 def trig_of(mix_ref, layer, group):
@@ -117,17 +110,18 @@
     for layer in range(2):
         trig = [trig_of(mix_ref, layer, group) for group in range(4)]
         for group, (cos, sin) in enumerate(trig):
-            tans[layer, group] = sin / cos
-        cut = trig[1][0] * trig[2][0] * trig[3][0]
+            if group in (1, 2):
+                tans[layer, group] = sin / cos
+        back = [(cos, -sin) for cos, sin in (trig[1], trig[3])]
+        cut = trig[1][0] * trig[2][0]
         cut = cut * cut
         cut = cut * cut
         scale = cut if scale is None else scale * cut
-        lanes_ref[layer] = lane_weights(lane_table(*trig[0]))
-        rows_ref[layer] = row_weights(row_table(*trig[1]))
+        lanes_ref[layer] = lane_weights(seven_bits(trig[0], trig[0]))
+        rows_ref[layer] = row_weights(seven_bits(back[0], back[1]))
     aux_ref[PHASE] = jnp.broadcast_to(phase_ref[1:2, :], (SUB, 128))
     aux_ref[SCALE] = scale
-    aux_ref[TAN2], aux_ref[TAN3] = tans[0, 2], tans[0, 3]
-    aux_ref[NEXT1], aux_ref[NEXT2], aux_ref[NEXT3] = tans[1, 1], tans[1, 2], tans[1, 3]
+    aux_ref[TAN2], aux_ref[NEXT1], aux_ref[NEXT2] = tans[0, 2], tans[1, 1], tans[1, 2]
     return tans[0, 1], tans[0, 2]
 
 
@@ -173,10 +167,10 @@
 
 def middle_kernel(aux_ref, lanes_ref, rows_ref, in_ref, out_ref, work_ref):
     angle, scale = aux_ref[PHASE], aux_ref[SCALE]
-    tan2, tan3, next2, next3 = aux_ref[TAN2], aux_ref[TAN3], aux_ref[NEXT2], aux_ref[NEXT3]
+    tan2, next2 = aux_ref[TAN2], aux_ref[NEXT2]
     lanes, rows = lanes_ref[0], rows_ref[0]
     for bank in range(4):
-        parts = [mix([in_ref[PLACE[bank * 16 + i], part] for i in range(16)], tan3) for part in range(2)]
+        parts = [[in_ref[PLACE[bank * 16 + i], part] for i in range(16)] for part in range(2)]
         parts = within(parts, lanes, rows)
         for part in range(2):
             for i in range(16):
@@ -197,7 +191,7 @@
     for bank in range(4):
         parts = within([[work_ref[bank, i, part] for i in range(16)] for part in range(2)], lanes, rows)
         for part in range(2):
-            for i, tile in enumerate(mix(parts[part], next3)):
+            for i, tile in enumerate(parts[part]):
                 out_ref[PLACE[bank * 16 + i], part] = tile
 
 

time: 66.4 us -> 66.3 us (level)
  no operation moved by 1% of the time
where the time goes in v6:
time: 66.3 us; the launch traced here: 66.1 us
  blocking collectives  62.2 us (94%)
  Pallas kernels  3.86 us (6%)
    all_to_all x2, blocking collectives, swap(): lax.all_to_all(values, ('bank', 'lane'), split_axis=0, concat_axis=0, axi...  62.2 us
    pallas_call x1, Pallas kernels, local(): pl.pallas_call(first_kernel, out_shape=(jax.ShapeDtypeStruct((64, 3, SUB,...  1.56 us
    pallas_call x1, Pallas kernels, local(): pl.pallas_call(middle_kernel, out_shape=jax.ShapeDtypeStruct((64, 2, SUB,...  1.39 us

profile of v6, /device:TPU:1, one launch (start us, length us, event | category | flops | bytes accessed | tf_op | source)
XLA Modules:
  0.0 66.1 jit_solution(6147740560534030752)
XLA Ops:
  0.0 1.6 %first.1 = (f32[64,3,8,128]{3,2,1,0:T(8,128)S(1)}, f32[5,8,128]{2,1,0:T(8,128)S(1)}, bf16[2,256,256]{2,1,0:T(8,128)(2,1)S(1)}, bf16[2,256,256]{2,1,0:T(8,128)(2,1)S(1)}) custom-call(f32[2,4]{1,0:T(2,128)} %mix_hbm.1, f32[2,128]{1,0:T(2,128)} %phase_hbm.1, f32[2,4,16,8,128]{4,3,2,1,0:T(8,128)} %bitcast.3, f32[4,16,8,128]{3,2,1,0:T(8,128)} %bitcast.4), custom_call_target="tpu_custom_call" | custom-call | tf_op jit(solution)/shard_map/first/pallas_call | solution.py:237
  1.6 37.1 %all_to_all.10.in_ref = f32[64,3,8,128]{3,2,1,0:T(8,128)S(1)} all-to-all(f32[64,3,8,128]{3,2,1,0:T(8,128)S(1)} %get-tuple-element.12), channel_id=1, replica_groups={{328,72,456,200,320,64,448,192,344,88,472,216,336,80,464,208,360,104,48..., dimensions={0} | all-to-all | bytes 1572864 | tf_op jit(solution)/shard_map/all_to_all | solution.py:222
  38.6 1.4 %middle.1 = f32[64,2,8,128]{3,2,1,0:T(8,128)S(1)} custom-call(f32[5,8,128]{2,1,0:T(8,128)S(1)} %get-tuple-element.9.aux_ref, bf16[2,256,256]{2,1,0:T(8,128)(2,1)S(1)} %get-tuple-element.10.lanes_ref, bf16[2,256,256]{2,1,0:T(8,128)(2,1)S(1)} %get-tuple-element.11.rows_ref, f32[64,3,8,128]{3,2,1,0:T(8,128)S(1)} %all_to_all.10.in_ref), custom_call_target="tpu_custom_call" | custom-call | tf_op jit(solution)/shard_map/middle/pallas_call | solution.py:257
  40.0 25.2 %all_to_all.11.in_ref = f32[64,2,8,128]{3,2,1,0:T(8,128)S(1)} all-to-all(f32[64,2,8,128]{3,2,1,0:T(8,128)S(1)} %middle.1), channel_id=1, replica_groups={{328,72,456,200,320,64,448,192,344,88,472,216,336,80,464,208,360,104,48..., dimensions={0} | all-to-all | bytes 1048576 | tf_op jit(solution)/shard_map/all_to_all | solution.py:222
  65.2 0.9 %last.1 = f32[2,4,16,8,128]{4,3,2,1,0:T(8,128)} custom-call(f32[5,8,128]{2,1,0:T(8,128)S(1)} %get-tuple-element.9.aux_ref, f32[64,2,8,128]{3,2,1,0:T(8,128)S(1)} %all_to_all.11.in_ref), custom_call_target="tpu_custom_call" | custom-call | tf_op jit(solution)/shard_map/last/pallas_call | solution.py:267

commit v7 on v6

--- a/solution.py
+++ b/solution.py
@@ -10,6 +10,8 @@
     bank * 16 + (y + 4) % 8 * 2 + 1 - core for y in range(8) for core in range(2) for bank in (2, 0, 3, 1)
 ]
 PLACE = [ORDER.index(k) for k in range(64)]
+BACK = [bank * 16 + (4 + 3 * k) % 8 * 2 + core for bank in (2, 0, 3, 1) for core in (1, 0) for k in range(8)]
+BACK_PLACE = [BACK.index(k) for k in range(64)]
 F32 = jnp.float32
 BF16 = jnp.bfloat16
 
@@ -192,14 +194,14 @@
         parts = within([[work_ref[bank, i, part] for i in range(16)] for part in range(2)], lanes, rows)
         for part in range(2):
             for i, tile in enumerate(parts[part]):
-                out_ref[PLACE[bank * 16 + i], part] = tile
+                out_ref[BACK_PLACE[bank * 16 + i], part] = tile
 
 
 def last_kernel(aux_ref, in_ref, out_hbm, work_ref, out_ref, sems):
     next1, next2 = aux_ref[NEXT1], aux_ref[NEXT2]
     for part in range(2):
         for i in range(16):
-            for b, tile in enumerate(mix([in_ref[b * 16 + i, part] for b in range(4)], next2)):
+            for b, tile in enumerate(mix([in_ref[BACK_PLACE[ORDER[b * 16 + i]], part] for b in range(4)], next2)):
                 work_ref[part, b, i] = tile
     copies = []
     for b in range(4):
@@ -218,9 +220,9 @@
 ROOM = pltpu.CompilerParams(vmem_limit_bytes=12 << 20)
 
 
-def swap(values):
+def swap(values, order=ORDER):
     return lax.all_to_all(
-        values, ("bank", "lane"), split_axis=0, concat_axis=0, axis_index_groups=[ORDER], tiled=True
+        values, ("bank", "lane"), split_axis=0, concat_axis=0, axis_index_groups=[order], tiled=True
     )
 
 
@@ -263,7 +265,7 @@
         compiler_params=ROOM,
         name="middle",
     )(aux, lanes, rows, held)
-    mine = swap(back)
+    mine = swap(back, BACK)
     out = pl.pallas_call(
         last_kernel,
         out_shape=jax.ShapeDtypeStruct((2, 4, 16, SUB, 128), F32),

time: 66.3 us -> 66.2 us (level)
  no operation moved by 1% of the time
where the time goes in v7:
time: 66.2 us; the launch traced here: 66.1 us
  blocking collectives  62.2 us (94%)
  Pallas kernels  3.88 us (6%)
    all_to_all x2, blocking collectives, swap(): lax.all_to_all(values, ('bank', 'lane'), split_axis=0, concat_axis=0, axi...  62.2 us
    pallas_call x1, Pallas kernels, local(): pl.pallas_call(first_kernel, out_shape=(jax.ShapeDtypeStruct((64, 3, SUB,...  1.56 us
    pallas_call x1, Pallas kernels, local(): pl.pallas_call(middle_kernel, out_shape=jax.ShapeDtypeStruct((64, 2, SUB,...  1.39 us

profile of v7, /device:TPU:1, one launch (start us, length us, event | category | flops | bytes accessed | tf_op | source)
XLA Modules:
  0.0 66.1 jit_solution(13687132754631003418)
XLA Ops:
  0.0 1.6 %first.1 = (f32[64,3,8,128]{3,2,1,0:T(8,128)S(1)}, f32[5,8,128]{2,1,0:T(8,128)S(1)}, bf16[2,256,256]{2,1,0:T(8,128)(2,1)S(1)}, bf16[2,256,256]{2,1,0:T(8,128)(2,1)S(1)}) custom-call(f32[2,4]{1,0:T(2,128)} %mix_hbm.1, f32[2,128]{1,0:T(2,128)} %phase_hbm.1, f32[2,4,16,8,128]{4,3,2,1,0:T(8,128)} %bitcast.3, f32[4,16,8,128]{3,2,1,0:T(8,128)} %bitcast.4), custom_call_target="tpu_custom_call" | custom-call | tf_op jit(solution)/shard_map/first/pallas_call | solution.py:239
  1.6 37.1 %all_to_all.10.in_ref = f32[64,3,8,128]{3,2,1,0:T(8,128)S(1)} all-to-all(f32[64,3,8,128]{3,2,1,0:T(8,128)S(1)} %get-tuple-element.12), channel_id=1, replica_groups={{328,72,456,200,320,64,448,192,344,88,472,216,336,80,464,208,360,104,48..., dimensions={0} | all-to-all | bytes 1572864 | tf_op jit(solution)/shard_map/all_to_all | solution.py:224
  38.6 1.4 %middle.1 = f32[64,2,8,128]{3,2,1,0:T(8,128)S(1)} custom-call(f32[5,8,128]{2,1,0:T(8,128)S(1)} %get-tuple-element.9.aux_ref, bf16[2,256,256]{2,1,0:T(8,128)(2,1)S(1)} %get-tuple-element.10.lanes_ref, bf16[2,256,256]{2,1,0:T(8,128)(2,1)S(1)} %get-tuple-element.11.rows_ref, f32[64,3,8,128]{3,2,1,0:T(8,128)S(1)} %all_to_all.10.in_ref), custom_call_target="tpu_custom_call" | custom-call | tf_op jit(solution)/shard_map/middle/pallas_call | solution.py:259
  40.0 25.1 %all_to_all.11.in_ref = f32[64,2,8,128]{3,2,1,0:T(8,128)S(1)} all-to-all(f32[64,2,8,128]{3,2,1,0:T(8,128)S(1)} %middle.1), channel_id=1, replica_groups={{328,376,296,344,264,312,360,280,320,368,288,336,256,304,352,272,72,120..., dimensions={0} | all-to-all | bytes 1048576 | tf_op jit(solution)/shard_map/all_to_all | solution.py:224
  65.1 0.9 %last.1 = f32[2,4,16,8,128]{4,3,2,1,0:T(8,128)} custom-call(f32[5,8,128]{2,1,0:T(8,128)S(1)} %get-tuple-element.9.aux_ref, f32[64,2,8,128]{3,2,1,0:T(8,128)S(1)} %all_to_all.11.in_ref), custom_call_target="tpu_custom_call" | custom-call | tf_op jit(solution)/shard_map/last/pallas_call | solution.py:269

commit v8 on v7

--- a/solution.py
+++ b/solution.py
@@ -208,9 +208,9 @@
         for part in range(2):
             for i, tile in enumerate(mix([work_ref[part, b, i] for i in range(16)], next1)):
                 out_ref[part, b, i] = tile
-        copy = pltpu.make_async_copy(out_ref.at[:, b], out_hbm.at[:, b], sems.at[b])
-        copy.start()
-        copies.append(copy)
+            copy = pltpu.make_async_copy(out_ref.at[part, b], out_hbm.at[part, b], sems.at[b * 2 + part])
+            copy.start()
+            copies.append(copy)
     for copy in copies:
         copy.wait()
 
@@ -274,7 +274,7 @@
         scratch_shapes=[
             pltpu.VMEM((2, 4, 16, SUB, 128), F32),
             pltpu.VMEM((2, 4, 16, SUB, 128), F32),
-            pltpu.SemaphoreType.DMA((4,)),
+            pltpu.SemaphoreType.DMA((8,)),
         ],
         compiler_params=ROOM,
         name="last",

time: 66.2 us -> 66.3 us (level)
  no operation moved by 1% of the time
where the time goes in v8:
time: 66.3 us; the launch traced here: 66.1 us
  blocking collectives  62.2 us (94%)
  Pallas kernels  3.92 us (6%)
    all_to_all x2, blocking collectives, swap(): lax.all_to_all(values, ('bank', 'lane'), split_axis=0, concat_axis=0, axi...  62.2 us
    pallas_call x1, Pallas kernels, local(): pl.pallas_call(first_kernel, out_shape=(jax.ShapeDtypeStruct((64, 3, SUB,...  1.56 us
    pallas_call x1, Pallas kernels, local(): pl.pallas_call(middle_kernel, out_shape=jax.ShapeDtypeStruct((64, 2, SUB,...  1.39 us

profile of v8, /device:TPU:1, one launch (start us, length us, event | category | flops | bytes accessed | tf_op | source)
XLA Modules:
  0.0 66.1 jit_solution(3757421117196416972)
XLA Ops:
  0.0 1.6 %first.1 = (f32[64,3,8,128]{3,2,1,0:T(8,128)S(1)}, f32[5,8,128]{2,1,0:T(8,128)S(1)}, bf16[2,256,256]{2,1,0:T(8,128)(2,1)S(1)}, bf16[2,256,256]{2,1,0:T(8,128)(2,1)S(1)}) custom-call(f32[2,4]{1,0:T(2,128)} %mix_hbm.1, f32[2,128]{1,0:T(2,128)} %phase_hbm.1, f32[2,4,16,8,128]{4,3,2,1,0:T(8,128)} %bitcast.3, f32[4,16,8,128]{3,2,1,0:T(8,128)} %bitcast.4), custom_call_target="tpu_custom_call" | custom-call | tf_op jit(solution)/shard_map/first/pallas_call | solution.py:239
  1.6 37.1 %all_to_all.10.in_ref = f32[64,3,8,128]{3,2,1,0:T(8,128)S(1)} all-to-all(f32[64,3,8,128]{3,2,1,0:T(8,128)S(1)} %get-tuple-element.12), channel_id=1, replica_groups={{328,72,456,200,320,64,448,192,344,88,472,216,336,80,464,208,360,104,48..., dimensions={0} | all-to-all | bytes 1572864 | tf_op jit(solution)/shard_map/all_to_all | solution.py:224
  38.6 1.4 %middle.1 = f32[64,2,8,128]{3,2,1,0:T(8,128)S(1)} custom-call(f32[5,8,128]{2,1,0:T(8,128)S(1)} %get-tuple-element.9.aux_ref, bf16[2,256,256]{2,1,0:T(8,128)(2,1)S(1)} %get-tuple-element.10.lanes_ref, bf16[2,256,256]{2,1,0:T(8,128)(2,1)S(1)} %get-tuple-element.11.rows_ref, f32[64,3,8,128]{3,2,1,0:T(8,128)S(1)} %all_to_all.10.in_ref), custom_call_target="tpu_custom_call" | custom-call | tf_op jit(solution)/shard_map/middle/pallas_call | solution.py:259
  40.0 25.1 %all_to_all.11.in_ref = f32[64,2,8,128]{3,2,1,0:T(8,128)S(1)} all-to-all(f32[64,2,8,128]{3,2,1,0:T(8,128)S(1)} %middle.1), channel_id=1, replica_groups={{328,376,296,344,264,312,360,280,320,368,288,336,256,304,352,272,72,120..., dimensions={0} | all-to-all | bytes 1048576 | tf_op jit(solution)/shard_map/all_to_all | solution.py:224
  65.1 1.0 %last.1 = f32[2,4,16,8,128]{4,3,2,1,0:T(8,128)} custom-call(f32[5,8,128]{2,1,0:T(8,128)S(1)} %get-tuple-element.9.aux_ref, f32[64,2,8,128]{3,2,1,0:T(8,128)S(1)} %all_to_all.11.in_ref), custom_call_target="tpu_custom_call" | custom-call | tf_op jit(solution)/shard_map/last/pallas_call | solution.py:269
